TPU v7x, 256 devices: a whole 4x4x8 slice. The times are simulated.
256 devices in a mesh: pts: 32 (over x, y, core), med: 8 (over z).
Axes of the slice: x: 4, y: 4, z: 8, core: 2. Of those that a mesh axis runs over, the one named last changes fastest.
Arguments:
- sketches: bfloat16 [32768, 4096], P('pts'), may hold values from -12 to 12
- assignment: int32 [32768], P('pts'), may hold values from 0 to 4095
- medoid_ids: int32 [4096], P('med'), may hold values from 0 to 32767, as said below
Outputs:
- gap: float32 [32768], P('pts')
- coverage: float32 [], replicated
- weights: float32 [4096], P('med')
- gradient_sums: float32 [4096, 4096], P('pts', 'med')
Inputs may be any that keep to these rules, and one draw needn't show every extreme that they name: `medoid_ids`: the 4096 medoid ids are distinct point indices.
All inputs are finite; a program needn't handle non-finite values.
Results may differ from a plain program's by a relative error of at most 0.0003.
Values may be sent and summed in bfloat16 or wider, within the bound.
No kernel may reach another device: no remote copies, remote signals or barrier semaphores. Data moves between devices by JAX's collectives and lax.ppermute only.
A program may use at most 64 MiB of HBM per device.

v0:
```python
import jax
import jax.numpy as jnp
from jax import lax
from jax.sharding import PartitionSpec as P


def from_everyone(array, axis):
    size = lax.axis_size(axis)
    return lax.all_to_all(
        jnp.broadcast_to(array[None], (size, *array.shape)), axis, 0, 0, tiled=True
    )


def over_copies(array, axis):
    return from_everyone(array, axis).sum(axis=0)


def together(arrays, axis):
    line, at, done = (jnp.concatenate([a.reshape(-1) for a in arrays]), 0, [])
    running = over_copies(line, axis)
    for a in arrays:
        done.append(running[at : at + a.size].reshape(a.shape))
        at += a.size
    return tuple(done)


def shards(sketches, assignment, medoid_ids):
    row_count, feat_width = sketches.shape
    medoid_count = medoid_ids.shape[0]
    pts_count = lax.axis_size("pts")
    pts_index = lax.axis_index("pts")
    med_index = lax.axis_index("med")
    medoid_iota = jnp.arange(medoid_count, dtype=jnp.int32)
    local_assign = assignment - med_index * medoid_count
    one_hot = (local_assign[:, None] == medoid_iota[None, :]).astype(jnp.bfloat16)
    offsets = medoid_ids - pts_index * row_count
    inside = (offsets >= 0) & (offsets < row_count)
    picked = jnp.take(sketches, jnp.clip(offsets, 0, row_count - 1), axis=0)
    fetch_terms = jnp.where(inside[:, None], picked, jnp.zeros_like(picked))
    medoid_slice = (
        lax.psum_scatter(fetch_terms, "pts", scatter_dimension=1, tiled=True)
        .astype(jnp.float32)
        .astype(jnp.bfloat16)
    )
    gradient_sums = lax.psum_scatter(
        lax.dot_general(
            sketches, one_hot, (((0,), (0,)), ((), ())), preferred_element_type=jnp.float32
        ),
        "pts",
        scatter_dimension=0,
        tiled=True,
    )
    count_terms = jnp.sum(one_hot.astype(jnp.float32), axis=0)
    raw_scores = lax.dot_general(
        sketches,
        lax.all_gather(medoid_slice, "pts", axis=1, tiled=True),
        (((1,), (1,)), ((), ())),
        preferred_element_type=jnp.float32,
    )
    scores = raw_scores * (1.0 / feat_width)
    best_local = jnp.max(scores, axis=1)
    in_shard = (local_assign >= 0) & (local_assign < medoid_count)
    taken = jnp.take_along_axis(
        scores, jnp.clip(local_assign, 0, medoid_count - 1)[:, None], axis=1
    )[:, 0]
    assigned_local = jnp.where(in_shard, taken, -1e30)
    best_score, assigned = lax.pmax((best_local, assigned_local), "med")
    gap = best_score - assigned
    weights, cover_total = together((count_terms, jnp.sum(best_score)), "pts")
    coverage = cover_total / (row_count * pts_count)
    return (gap, coverage, weights, gradient_sums)


def solution(mesh):
    in_specs = (P("pts", None), P("pts"), P("med"))
    out_specs = (P("pts"), P(), P("med"), P("pts", "med"))
    return jax.shard_map(shards, mesh=mesh, in_specs=in_specs, out_specs=out_specs, check_vma=False)
```

profile of v0, /device:TPU:2, one launch (start us, length us, event | category | flops | bytes accessed | tf_op | source)
XLA Modules:
  0.0 295.6 jit_solution(7401411365770368771)
XLA Ops:
  7.2 0.0 reduce-scatter.7.cloned.1.call-start
  7.2 0.7 compare_and_fusion
  7.9 13.1 %gather_fusion = bf16[512,4096]{1,0:T(8,128)(2,1)} fusion(bf16[1024,4096]{1,0:T(8,128)(2,1)} %param.3, s32[1024]{0:T(1024)S(1)} %pad_clamp_fusion), kind=kCustom, calls=%fused_computation | custom fusion | bytes 8390656 | tf_op jit(solution)/shard_map/jit(_take)/gather | solution.py:38
  21.0 4.0 %select_select_fusion = bf16[512,4096]{1,0:T(8,128)(2,1)} fusion(bf16[512,4096]{1,0:T(8,128)(2,1)} %gather_fusion, pred[512]{0:T(512)(128)(4,1)S(1)} %get-tuple-element.28, pred[512]{0:T(512)(128)(4,1)S(1)} %get-tuple-element.34), kind=kLoop, calls=%fused_computation.3 | loop fusion | flops 4194304 | bytes 8389632 | tf_op jit(solution)/shard_map/jit(_where)/select_n | solution.py:39
  25.0 6.5 %copy.13 = bf16[512,4096]{0,1:T(8,128)(2,1)} copy(bf16[512,4096]{1,0:T(8,128)(2,1)} %select_select_fusion) | data formatting | bytes 8388608
  31.4 0.0 copy-start
  31.4 0.0 reduce-scatter.7.cloned.1.call-update
  31.5 0.0 all-gather.2.cloned.1.call-start
  31.5 92.7 %reduce-scatter.7.cloned.1.call-done = bf16[128,512]{1,0:T(8,128)(2,1)} async-done(((bf16[4096,512]{1,0:T(8,128)(2,1)}), bf16[128,512]{1,0:T(8,128)(2,1)}) %reduce-scatter.7.cloned.1.call-update) | async-done | bytes 131088
  124.2 1.7 copy.14
  125.9 0.0 all-gather.2.cloned.1.call-update
  125.9 0.0 reduce-scatter.5.cloned.1.call-start
  126.0 0.0 copy-done
  126.0 10.4 %convolution_bitcast_fusion = f32[4096,512]{0,1:T(8,128)} fusion(bf16[1024,4096]{1,0:T(8,128)(2,1)} %param.3, s32[1024]{0:T(1024)S(1)} %get-tuple-element.27), kind=kOutput, calls=%fused_computation.2 | convolution fusion | flops 4295491584 | bytes 16781312 | tf_op jit(solution)/shard_map/dot_general | solution.py:46
  136.4 0.0 reduce-scatter.5.cloned.1.call-update
  136.4 0.3 convert_reduce_fusion
  136.7 43.6 %all-gather.2.cloned.1.call-done = bf16[512,4096]{1,0:T(8,128)(2,1)} async-done(((bf16[512,128]{1,0:T(8,128)(2,1)}), bf16[512,4096]{1,0:T(8,128)(2,1)}) %all-gather.2.cloned.1.call-update) | async-done | bytes 4194320 | tf_op jit(solution)/shard_map/all_gather | solution.py:56
  180.3 8.3 %multiply_bitcast_fusion = (f32[1024,512]{0,1:T(8,128)S(1)}, f32[1024]{0:T(1024)S(1)}) fusion(bf16[512,4096]{1,0:T(8,128)(2,1)} %all-gather.2.cloned.1.call-done, bf16[1024,4096]{1,0:T(8,128)(2,1)} %param.3), kind=kOutput, calls=%fused_computation.7 | convolution fusion | flops 4296014848 | bytes 14684160 | tf_op jit(solution)/shard_map/dot_general | solution.py:54
  188.6 8.6 %gather_fusion.1 = f32[1024]{0:T(1024)S(1)} fusion(f32[1024,512]{0,1:T(8,128)S(1)} %get-tuple-element.30, s32[1024]{0:T(1024)S(1)} %bitcast.15), kind=kCustom, calls=%fused_computation.1 | custom fusion | bytes 16384 | tf_op jit(solution)/shard_map/jit(take_along_axis)/gather | solution.py:63
  197.2 17.7 %all-reduce = (f32[1024]{0:T(1024)S(1)}, f32[1024]{0:T(1024)S(1)}) all-reduce(f32[1024]{0:T(1024)S(1)} %get-tuple-element.31, f32[1024]{0:T(1024)S(1)} %select_select_fusion.1), channel_id=1, replica_groups=mesh['pts'=32,'med'=8] {'med'}, use_global_device_ids=true, to_apply=%region_2.3 | all-reduce | flops 2048 | bytes 16384 | tf_op jit(solution)/shard_map/pmax | solution.py:67
  215.0 1.2 fusion.5
  216.2 0.7 pad_maximum_fusion
  216.8 0.7 broadcast_in_dim.48
  217.5 6.0 %all-to-all-start = ((f32[32,1,513]{2,1,0:T(1,128)}), f32[32,1,513]{2,1,0:T(1,128)S(1)}, u32[]{:S(2)}, u32[]{:S(2)}) async-start(f32[32,1,513]{2,1,0:T(1,128)} %broadcast_in_dim.48), calls=%async_computation | async-start | bytes 163840 | tf_op jit(solution)/shard_map/all_to_all | solution.py:9
  223.5 60.8 %reduce-scatter.5.cloned.1.call-done = f32[128,512]{0,1:T(8,128)} async-done(((f32[4096,512]{0,1:T(8,128)}), f32[128,512]{0,1:T(8,128)}) %reduce-scatter.5.cloned.1.call-update) | async-done | bytes 262160 | tf_op jit(solution)/shard_map/reduce_scatter | solution.py:45
  284.3 1.8 copy.12
  286.1 0.0 all-to-all-done
  286.1 0.1 reduce_sum.29
  286.2 0.5 slice.6
  286.7 0.6 slice.7
  (6 shorter events, 0.1 us)
Async XLA Ops:
  7.2 117.1 %reduce-scatter.7.cloned.1.call-start = ((), (), s32[]{:S(2)}) async-start(), calls=%async_computation.5 | async-start | bytes 4325376
  31.4 94.5 %copy-start = (s32[1024]{0:T(1024)S(1)}, s32[1024]{0:T(1024)}, u32[]{:S(2)}) copy-start(s32[1024]{0:T(1024)} %param.4) | copy-start | bytes 12292
  31.5 148.8 %all-gather.2.cloned.1.call-start = ((), (), s32[]{:S(2)}) async-start(), calls=%async_computation.3 | async-start | bytes 4325376 | tf_op jit(solution)/shard_map/all_gather | solution.py:56
  125.9 158.4 %reduce-scatter.5.cloned.1.call-start = ((), (), s32[]{:S(2)}) async-start(), calls=%async_computation.4 | async-start | bytes 8650752 | tf_op jit(solution)/shard_map/reduce_scatter | solution.py:45
  217.5 68.6 %all-to-all-start = ((f32[32,1,513]{2,1,0:T(1,128)}), f32[32,1,513]{2,1,0:T(1,128)S(1)}, u32[]{:S(2)}, u32[]{:S(2)}) async-start(f32[32,1,513]{2,1,0:T(1,128)} %broadcast_in_dim.48), calls=%async_computation | async-start | bytes 163840 | tf_op jit(solution)/shard_map/all_to_all | solution.py:9
Sparse Core Ops, SparseCore 0:
  31.6 92.5 reduce-scatter.6
  127.3 52.9 all-gather.1
  184.3 99.9 reduce-scatter.4
where the time goes:
time: 296 us
  waiting for transfers between devices  197 us (67%)
  local copies, waits for them, and re-layouts  33.4 us (11%)
  matrix products  18.6 us (6%)
  blocking collectives  17.7 us (6%)
  between operations  15.6 us (5%)
  other arithmetic  6.93 us (2%)
  starting transfers between devices  6.15 us (2%)
    unnamed x4, waiting for transfers between devices  92.8 us
    reduce_scatter x1, waiting for transfers between devices, shards(): lax.psum_scatter(lax.dot_general(sketches, one_hot, (((0,), (0,)), ((), (...  60.8 us
    all_gather x1, waiting for transfers between devices, shards(): lax.all_gather(medoid_slice, 'pts', axis=1, tiled=True)  43.6 us
    pmax x1, blocking collectives, shards(): best_score, assigned = lax.pmax((best_local, assigned_local), 'med')  17.7 us
    gather x1, local copies, waits for them, and re-layouts, shards(): picked = jnp.take(sketches, jnp.clip(offsets, 0, row_count - 1), axis=0)  13.1 us
    dot_general x1, matrix products, shards(): lax.dot_general(sketches, one_hot, (((0,), (0,)), ((), ())), preferred_el...  10.4 us
    unnamed x6, local copies, waits for them, and re-layouts  9.92 us
    gather x1, local copies, waits for them, and re-layouts, shards(): jnp.take_along_axis(scores, jnp.clip(local_assign, 0, medoid_count - 1)[:...  8.65 us
  transfers between devices with their start and end apart: 4, of which 3 were waited for; matrix products, arithmetic and copies ran while one was open for 11% of the time, Pallas kernels for 0%

commit v1 on v0

--- a/solution.py
+++ b/solution.py
@@ -2,6 +2,13 @@
 import jax.numpy as jnp
 from jax import lax
 from jax.sharding import PartitionSpec as P
+
+
+def keep_up_signs(xin, comm_axis, join_dim):
+    step_out = jax.lax.axis_size(comm_axis)
+    r_now = jnp.concatenate(step_out * [xin], join_dim)
+    lower = jax.lax.all_to_all(r_now, comm_axis, join_dim, join_dim, tiled=True)
+    return lower
 
 
 def from_everyone(array, axis):
@@ -53,7 +60,7 @@
     count_terms = jnp.sum(one_hot.astype(jnp.float32), axis=0)
     raw_scores = lax.dot_general(
         sketches,
-        lax.all_gather(medoid_slice, "pts", axis=1, tiled=True),
+        keep_up_signs(medoid_slice, "pts", 1),
         (((1,), (1,)), ((), ())),
         preferred_element_type=jnp.float32,
     )

time: 296 us -> 262 us (0.89)
  waiting for transfers between devices: 197 us -> 133 us
  blocking collectives: 17.7 us -> 35.3 us
  local copies, waits for them, and re-layouts: 33.4 us -> 43.6 us
    reduce_scatter x1, waiting for transfers between devices: 60.8 us -> 0.02 us  [shards(): lax.psum_scatter(lax.dot_general(sketches, one_hot, (((0,), (0,)), ((), (...]
    all_to_all x1, waiting for transfers between devices: 0.01 us -> 50.8 us  [keep_up_signs(): lower = jax.lax.all_to_all(r_now, comm_axis, join_dim, join_dim, tiled=True)]
    all_gather x1 -> x0, waiting for transfers between devices: 43.6 us -> none  [shards(): lax.all_gather(medoid_slice, 'pts', axis=1, tiled=True)]
    all_to_all x0 -> x1, blocking collectives: none -> 17.6 us  [from_everyone(): lax.all_to_all(jnp.broadcast_to(array[None], (size, *array.shape)), axis,...]
    unnamed x4 -> x3, waiting for transfers between devices: 92.8 us -> 81.7 us
    all_to_all x0 -> x2, local copies, waits for them, and re-layouts: none -> 9.62 us  [keep_up_signs(): lower = jax.lax.all_to_all(r_now, comm_axis, join_dim, join_dim, tiled=True)]
    unnamed x6 -> x37, local copies, waits for them, and re-layouts: 9.92 us -> 11.1 us
  transfers between devices with their start and end apart: 4 -> 3, of which waited for: 3 -> 2; matrix products, arithmetic and copies ran while one was open for 11% -> 16% of each run, Pallas kernels for 0% -> 0%
where the time goes in v1:
time: 262 us; the launch traced here: 259 us
  waiting for transfers between devices  133 us (51%)
  local copies, waits for them, and re-layouts  43.6 us (17%)
  blocking collectives  35.3 us (13%)
  matrix products  18.8 us (7%)
  between operations  16.2 us (6%)
  other arithmetic  6.88 us (3%)
  starting transfers between devices  5.98 us (2%)
    unnamed x3, waiting for transfers between devices  81.7 us
    all_to_all x1, waiting for transfers between devices, keep_up_signs(): lower = jax.lax.all_to_all(r_now, comm_axis, join_dim, join_dim, tiled=True)  50.8 us
    pmax x1, blocking collectives, shards(): best_score, assigned = lax.pmax((best_local, assigned_local), 'med')  17.7 us
    all_to_all x1, blocking collectives, from_everyone(): lax.all_to_all(jnp.broadcast_to(array[None], (size, *array.shape)), axis,...  17.6 us
    gather x1, local copies, waits for them, and re-layouts, shards(): picked = jnp.take(sketches, jnp.clip(offsets, 0, row_count - 1), axis=0)  13 us
    unnamed x37, local copies, waits for them, and re-layouts  11.1 us
    dot_general x1, matrix products, shards(): lax.dot_general(sketches, one_hot, (((0,), (0,)), ((), ())), preferred_el...  10.4 us
    all_to_all x2, local copies, waits for them, and re-layouts, keep_up_signs(): lower = jax.lax.all_to_all(r_now, comm_axis, join_dim, join_dim, tiled=True)  9.62 us
  transfers between devices with their start and end apart: 3, of which 2 were waited for; matrix products, arithmetic and copies ran while one was open for 16% of the time, Pallas kernels for 0%

profile of v1, /device:TPU:2, one launch (start us, length us, event | category | flops | bytes accessed | tf_op | source)
XLA Modules:
  0.0 259.3 jit_solution(9608430654124263275)
XLA Ops:
  7.2 0.0 reduce-scatter.7.cloned.1.call-start
  7.2 0.7 compare_and_fusion
  7.9 13.0 %gather_fusion = bf16[512,4096]{1,0:T(8,128)(2,1)} fusion(bf16[1024,4096]{1,0:T(8,128)(2,1)} %param.3, s32[1024]{0:T(1024)S(1)} %pad_clamp_fusion), kind=kCustom, calls=%fused_computation | custom fusion | bytes 8390656 | tf_op jit(solution)/shard_map/jit(_take)/gather | solution.py:45
  20.9 3.9 %select_select_fusion = bf16[512,4096]{1,0:T(8,128)(2,1)} fusion(bf16[512,4096]{1,0:T(8,128)(2,1)} %gather_fusion, pred[512]{0:T(512)(128)(4,1)S(1)} %get-tuple-element.32, pred[512]{0:T(512)(128)(4,1)S(1)} %get-tuple-element.38), kind=kLoop, calls=%fused_computation.4 | loop fusion | flops 4194304 | bytes 8389632 | tf_op jit(solution)/shard_map/jit(_where)/select_n | solution.py:46
  24.9 6.5 %copy.21 = bf16[512,4096]{0,1:T(8,128)(2,1)} copy(bf16[512,4096]{1,0:T(8,128)(2,1)} %select_select_fusion) | data formatting | bytes 8388608
  31.4 0.0 copy-start
  31.4 0.0 reduce-scatter.7.cloned.1.call-update
  31.4 0.0 reduce-scatter.5.cloned.1.call-start
  31.5 0.6 copy-done
  32.1 10.4 %convolution_bitcast_fusion = f32[4096,512]{0,1:T(8,128)} fusion(bf16[1024,4096]{1,0:T(8,128)(2,1)} %param.3, s32[1024]{0:T(1024)S(1)} %get-tuple-element.31), kind=kOutput, calls=%fused_computation.2 | convolution fusion | flops 4295491584 | bytes 16781312 | tf_op jit(solution)/shard_map/dot_general | solution.py:53
  42.4 0.0 reduce-scatter.5.cloned.1.call-update
  42.5 81.7 %reduce-scatter.7.cloned.1.call-done = bf16[128,512]{1,0:T(8,128)(2,1)} async-done(((bf16[4096,512]{1,0:T(8,128)(2,1)}), bf16[128,512]{1,0:T(8,128)(2,1)}) %reduce-scatter.7.cloned.1.call-update) | async-done | bytes 131088
  124.2 1.0 copy.22
  126.7 3.1 %copy_bitcast_fusion = bf16[512,32,128]{2,0,1:T(8,128)(2,1)} fusion(bf16[512,4096]{1,0:T(8,128)(2,1)S(1)} %constant_dynamic-update-slice_fusion), kind=kLoop, calls=%fused_computation.3 | loop fusion | bytes 8388608 | tf_op jit(solution)/shard_map/all_to_all | solution.py:10
  129.8 5.9 %all-to-all-start = ((bf16[512,32,128]{2,0,1:T(8,128)(2,1)}), bf16[512,32,128]{2,0,1:T(8,128)(2,1)}, u32[]{:S(2)}, u32[]{:S(2)}) async-start(bf16[512,32,128]{2,0,1:T(8,128)(2,1)} %copy_bitcast_fusion), calls=%async_computation | async-start | bytes 8388608 | tf_op jit(solution)/shard_map/all_to_all | solution.py:10
  135.8 0.3 convert_reduce_fusion
  136.1 50.8 %all-to-all-done = bf16[512,32,128]{2,0,1:T(8,128)(2,1)} async-done(((bf16[512,32,128]{2,0,1:T(8,128)(2,1)}), bf16[512,32,128]{2,0,1:T(8,128)(2,1)}, u32[]{:S(2)}, u32[]{:S(2)}) %all-to-all-start) | async-done | bytes 4194336 | tf_op jit(solution)/shard_map/all_to_all | solution.py:10
  186.9 6.5 %copy.18 = bf16[512,32,128]{0,2,1:T(8,128)(2,1)} copy(bf16[512,32,128]{2,0,1:T(8,128)(2,1)} %all-to-all-done) | data formatting | bytes 8388608 | tf_op jit(solution)/shard_map/all_to_all | solution.py:10
  193.4 8.5 %multiply_bitcast_fusion = (f32[1024,512]{0,1:T(8,128)S(1)}, f32[1024]{0:T(1024)S(1)}) fusion(bf16[512,4096]{0,1:T(8,128)(2,1)} %bitcast.23, bf16[1024,4096]{1,0:T(8,128)(2,1)} %param.3), kind=kOutput, calls=%fused_computation.8 | convolution fusion | flops 4296014848 | bytes 14684160 | tf_op jit(solution)/shard_map/dot_general | solution.py:61
  201.8 8.6 %gather_fusion.1 = f32[1024]{0:T(1024)S(1)} fusion(f32[1024,512]{0,1:T(8,128)S(1)} %get-tuple-element.34, s32[1024]{0:T(1024)S(1)} %bitcast.21), kind=kCustom, calls=%fused_computation.1 | custom fusion | bytes 16384 | tf_op jit(solution)/shard_map/jit(take_along_axis)/gather | solution.py:70
  210.5 17.7 %all-reduce = (f32[1024]{0:T(1024)S(1)}, f32[1024]{0:T(1024)S(1)}) all-reduce(f32[1024]{0:T(1024)S(1)} %get-tuple-element.35, f32[1024]{0:T(1024)S(1)} %select_select_fusion.1), channel_id=1, replica_groups=mesh['pts'=32,'med'=8] {'med'}, use_global_device_ids=true, to_apply=%region_2.3 | all-reduce | flops 2048 | bytes 16384 | tf_op jit(solution)/shard_map/pmax | solution.py:74
  228.2 1.2 fusion.5
  229.4 0.7 pad_maximum_fusion
  230.1 17.6 %all_to_all.18 = f32[32,1,513]{2,1,0:T(1,128)S(1)} all-to-all(f32[32,1,513]{2,1,0:T(1,128)S(1)} %broadcast_in_dim.48), channel_id=1, replica_groups=mesh['pts'=32,'med'=8] {'pts'}, dimensions={0} | all-to-all | bytes 131328 | tf_op jit(solution)/shard_map/all_to_all | solution.py:16
  247.7 0.1 reduce_sum.29
  247.8 0.5 slice.6
  248.3 0.6 slice.7
  249.5 0.0 reduce-scatter.5.cloned.1.call-done
  249.5 1.8 copy.20
  (39 shorter events, 1.3 us)
Async XLA Ops:
  7.2 117.0 %reduce-scatter.7.cloned.1.call-start = ((), (), s32[]{:S(2)}) async-start(), calls=%async_computation.5 | async-start | bytes 4325376
  31.4 0.7 copy-start
  31.4 218.1 %reduce-scatter.5.cloned.1.call-start = ((), (), s32[]{:S(2)}) async-start(), calls=%async_computation.4 | async-start | bytes 8650752 | tf_op jit(solution)/shard_map/reduce_scatter | solution.py:52
  129.8 57.0 %all-to-all-start = ((bf16[512,32,128]{2,0,1:T(8,128)(2,1)}), bf16[512,32,128]{2,0,1:T(8,128)(2,1)}, u32[]{:S(2)}, u32[]{:S(2)}) async-start(bf16[512,32,128]{2,0,1:T(8,128)(2,1)} %copy_bitcast_fusion), calls=%async_computation | async-start | bytes 8388608 | tf_op jit(solution)/shard_map/all_to_all | solution.py:10
Sparse Core Ops, SparseCore 0:
  31.5 92.5 reduce-scatter.6
  128.2 101.9 reduce-scatter.4
